TPU v7x, 32 devices: a whole 2x2x4 slice. The times are simulated.
32 devices in a mesh: dp: 4 (over y, core), expert: 4 (over z), tensor: 2 (over x).
Axes of the slice: x: 2, y: 2, z: 4, core: 2. Of those that a mesh axis runs over, the one named last changes fastest.
Arguments:
- router_input: bfloat16 [1024, 2048], P(('dp', 'expert'), 'tensor'), may hold values from -6 to 6
- router_weight: bfloat16 [2048, 8], replicated, may hold values from -0.125 to 0.125
- expert_ids: int32 [1024, 2], P(('dp', 'expert', 'tensor')), may hold values from 0 to 7, all different within a row; in each aligned block of 32 rows (0 to 31, 32 to 63, ...) at most 9 rows name the same one
- down_weight: bfloat16 [61440, 2048], P(('expert', 'tensor')), may hold values from -0.0625 to 0.0625
- hidden: bfloat16 [4, 72, 61440], P('dp', None, ('expert', 'tensor')), may hold values from -6 to 6
- grad_output: bfloat16 [1024, 2048], P(('dp', 'expert', 'tensor')), may hold values from -4 to 4
Outputs:
- weight_grad: bfloat16 [61440, 2048], P(('expert', 'tensor', 'dp'))
- hidden_grad: bfloat16 [4, 72, 61440], P('dp', None, ('expert', 'tensor'))
- router_grad: float32 [2048, 8], replicated
- input_grad: bfloat16 [1024, 2048], P(('dp', 'expert', 'tensor'))
Inputs may be any that keep to these rules, and one draw needn't show every extreme that they name: `expert_ids`: each row names 2 different experts. Within the 32 rows of one device no expert is named more than 9 times, and some device's rows name some expert exactly 9 times.
All inputs are finite; a program needn't handle non-finite values.
Results may differ from a plain program's by a relative error of at most 0.018.
Values may be sent and summed in bfloat16 or wider, within the bound.
A program may use at most 192 MiB of HBM per device.

v0:
```python
import jax
import jax.numpy as jnp
from jax import lax
from jax.sharding import PartitionSpec as P


def per_device(router_input, router_weight, expert_ids, down_weight, hidden, grad_output):
    token_rows = grad_output.shape[0]
    model_width = grad_output.shape[1]
    expert_count = router_weight.shape[1]
    choose_count = expert_ids.shape[1]
    expert_ranks = lax.axis_size("expert")
    tensor_ranks = lax.axis_size("tensor")
    sources = expert_ranks * tensor_ranks
    spread = sources // expert_count
    capacity = hidden.shape[1] // sources
    full_input = lax.all_to_all(router_input, "tensor", split_axis=0, concat_axis=1, tiled=True)
    logits = jnp.dot(full_input, router_weight, preferred_element_type=jnp.float32)
    labels = jnp.arange(expert_count, dtype=jnp.int32)
    onehot_int = (expert_ids[:, :, None] == labels).astype(jnp.int32)
    onehot = onehot_int.astype(jnp.float32)
    picked = jnp.sum(onehot * logits[:, None, :], axis=2)
    first_gate = jax.nn.sigmoid(picked[:, 0] - picked[:, 1])
    second_gate = jax.nn.sigmoid(picked[:, 1] - picked[:, 0])
    gate_values = jnp.stack([first_gate, second_gate], axis=1)
    gate_low = gate_values.astype(jnp.bfloat16)
    flat_hits = onehot_int.reshape(token_rows * choose_count, expert_count)
    before = jnp.cumsum(flat_hits, axis=0) - flat_hits
    slot_pos = jnp.sum(before * flat_hits, axis=1).reshape(token_rows, choose_count)
    slot_ids = jnp.arange(capacity, dtype=jnp.int32)
    dispatch_table = onehot[:, :, :, None] * (slot_pos[:, :, None, None] == slot_ids).astype(
        jnp.float32
    )
    slot_table = jnp.sum(dispatch_table, axis=1).astype(jnp.bfloat16)
    packed_grad = jnp.einsum(
        "rec,rd->ecd", slot_table, grad_output, preferred_element_type=jnp.float32
    ).astype(jnp.bfloat16)
    packed_gate = jnp.einsum("rkec,rk->ec", dispatch_table, gate_low.astype(jnp.float32)).astype(
        jnp.bfloat16
    )
    send_grad = jnp.repeat(packed_grad, spread, axis=0)
    send_gate = jnp.repeat(packed_gate, spread, axis=0)
    recv_grad, recv_gate = (
        lax.all_to_all(send_grad, ("expert", "tensor"), split_axis=0, concat_axis=0, tiled=True),
        lax.all_to_all(send_gate, ("expert", "tensor"), split_axis=0, concat_axis=0, tiled=True),
    )
    recv_grad = recv_grad.reshape(sources * capacity, model_width)
    recv_gate = recv_gate.reshape(sources * capacity).astype(jnp.float32)
    hidden_rows = hidden[0]
    gated_grad = (recv_gate[:, None] * recv_grad.astype(jnp.float32)).astype(jnp.bfloat16)
    expert_image = lax.dot_general(
        recv_grad, down_weight, (((1,), (1,)), ((), ())), preferred_element_type=jnp.float32
    )
    hidden_part = (recv_gate[:, None] * expert_image).astype(jnp.bfloat16)
    gate_partial = jnp.sum(hidden_rows.astype(jnp.float32) * expert_image, axis=1).reshape(
        sources, capacity
    )
    returned = lax.all_to_all(
        gate_partial, ("expert", "tensor"), split_axis=0, concat_axis=0, tiled=True
    )
    expert_sums = jnp.sum(returned.reshape(expert_count, spread, capacity), axis=1)
    gate_grad = jnp.einsum("rkec,ec->rk", dispatch_table, expert_sums)
    mixed_term = jnp.sum(gate_values * gate_grad, axis=1, keepdims=True)
    logit_part = gate_values * (gate_grad - mixed_term)
    logit_grad = jnp.sum(onehot * logit_part[:, :, None], axis=1)
    input_grad = jnp.dot(
        logit_grad, router_weight.astype(jnp.float32).T, precision=lax.Precision.HIGHEST
    ).astype(jnp.bfloat16)
    router_local = jnp.dot(
        full_input.astype(jnp.float32).T, logit_grad, precision=lax.Precision.HIGHEST
    )
    router_grad = lax.psum(router_local, ("dp", "expert", "tensor"))
    hidden_all = lax.all_to_all(hidden_rows, "dp", split_axis=1, concat_axis=0, tiled=True)
    gated_all = lax.all_gather(gated_grad, "dp", axis=0, tiled=True)
    weight_sum = lax.dot_general(
        hidden_all, gated_all, (((0,), (0,)), ((), ())), preferred_element_type=jnp.float32
    ).astype(jnp.bfloat16)
    return (weight_sum, hidden_part[None], router_grad, input_grad)


def solution(mesh):
    return jax.shard_map(
        per_device,
        mesh=mesh,
        in_specs=(
            P(("dp", "expert"), "tensor"),
            P(),
            P(("dp", "expert", "tensor"), None),
            P(("expert", "tensor"), None),
            P("dp", None, ("expert", "tensor")),
            P(("dp", "expert", "tensor"), None),
        ),
        out_specs=(
            P(("expert", "tensor", "dp"), None),
            P("dp", None, ("expert", "tensor")),
            P(),
            P(("dp", "expert", "tensor"), None),
        ),
        check_vma=False,
    )
```

profile of v0, /device:TPU:1, one launch (start us, length us, event | category | flops | bytes accessed | tf_op | source)
XLA Modules:
  0.0 211.5 jit_solution(2945085626296198110)
XLA Ops:
  8.0 3.5 %all-to-all-start = ((bf16[2,32,1024]{2,1,0:T(8,128)(2,1)}), bf16[2,32,1024]{2,1,0:T(8,128)(2,1)S(1)}, u32[]{:S(2)}, u32[]{:S(2)}) async-start(bf16[2,32,1024]{2,1,0:T(8,128)(2,1)} %bitcast.51), calls=%async_computation | async-start | bytes 262144 | tf_op jit(solution)/shard_map/all_to_all | solution.py:17
  11.5 0.8 copy.34
  12.3 0.7 convert_convert_fusion
  13.2 0.1 reduce_window_sum.11
  13.3 0.2 select_reduce_fusion
  13.4 0.1 eq.53
  13.7 1.7 all-to-all-done
  15.4 0.9 fusion.14
  16.3 0.7 multiply_reduce_fusion.2
  17.1 0.2 fusion.2
  17.4 0.6 copy.37
  18.0 4.9 %all-to-all-start.1 = ((bf16[8,1,9]{2,1,0:T(2,128)(2,1)}), bf16[8,1,9]{2,1,0:T(2,128)(2,1)S(1)}, u32[]{:S(2)}, u32[]{:S(2)}) async-start(bf16[8,1,9]{2,1,0:T(2,128)(2,1)} %copy.37), calls=%async_computation.1 | async-start | bytes 8192 | tf_op jit(solution)/shard_map/all_to_all | solution.py:45
  22.8 1.1 convolution_convert_fusion
  23.9 4.2 %all-to-all-done.1 = bf16[8,1,9]{2,1,0:T(2,128)(2,1)S(1)} async-done(((bf16[8,1,9]{2,1,0:T(2,128)(2,1)}), bf16[8,1,9]{2,1,0:T(2,128)(2,1)S(1)}, u32[]{:S(2)}, u32[]{:S(2)}) %all-to-all-start.1) | async-done | bytes 176 | tf_op jit(solution)/shard_map/all_to_all | solution.py:45
  28.1 3.5 %all-to-all-start.2 = ((bf16[8,9,2048]{2,1,0:T(8,128)(2,1)}), bf16[8,9,2048]{2,1,0:T(8,128)(2,1)S(1)}, u32[]{:S(2)}, u32[]{:S(2)}) async-start(bf16[8,9,2048]{2,1,0:T(8,128)(2,1)} %convolution_convert_fusion), calls=%async_computation.2 | async-start | bytes 1048576 | tf_op jit(solution)/shard_map/all_to_all | solution.py:44
  31.7 10.3 %all-to-all-done.2 = bf16[8,9,2048]{2,1,0:T(8,128)(2,1)S(1)} async-done(((bf16[8,9,2048]{2,1,0:T(8,128)(2,1)}), bf16[8,9,2048]{2,1,0:T(8,128)(2,1)S(1)}, u32[]{:S(2)}, u32[]{:S(2)}) %all-to-all-start.2) | async-done | bytes 294944 | tf_op jit(solution)/shard_map/all_to_all | solution.py:44
  42.0 0.1 reshape.60
  42.2 0.8 multiply_convert_fusion.1
  43.0 15.7 %fusion = (f32[72]{0:T(128)S(1)}, bf16[1,72,7680]{2,1,0:T(8,128)(2,1)}) fusion(bf16[1,72,7680]{2,1,0:T(8,128)(2,1)S(1)} %copy-done.1, f32[72]{0:T(128)S(1)} %reshape.61, bf16[72,2048]{1,0:T(8,128)(2,1)S(1)} %reshape.60, bf16[7680,2048]{1,0:T(8,128)(2,1)} %param.9), kind=kOutput, calls=%fused_computation.5 | convolution fusion | flops 2267688960 | bytes 33964608 | tf_op jit(solution)/shard_map/dot_general | solution.py:51
  58.8 0.7 all_to_all.54
  59.5 6.6 %all-to-all-start.4 = ((f32[8,1,9]{2,1,0:T(1,128)}), f32[8,1,9]{2,1,0:T(1,128)S(1)}, u32[]{:S(2)}, u32[]{:S(2)}) async-start(f32[8,1,9]{2,1,0:T(1,128)} %bitcast.13), calls=%async_computation.4 | async-start | bytes 8192 | tf_op jit(solution)/shard_map/all_to_all | solution.py:58
  66.0 0.3 all_to_all.50
  66.4 1.1 copy.39
  67.5 3.8 %all-to-all-done.4 = f32[8,1,9]{2,1,0:T(1,128)S(1)} async-done(((f32[8,1,9]{2,1,0:T(1,128)}), f32[8,1,9]{2,1,0:T(1,128)S(1)}, u32[]{:S(2)}, u32[]{:S(2)}) %all-to-all-start.4) | async-done | bytes 320 | tf_op jit(solution)/shard_map/all_to_all | solution.py:58
  71.3 6.7 %all-to-all-start.3 = ((bf16[72,4,1920]{2,0,1:T(8,128)(2,1)}), bf16[72,4,1920]{2,0,1:T(8,128)(2,1)S(1)}, u32[]{:S(2)}, u32[]{:S(2)}) async-start(bf16[72,4,1920]{2,0,1:T(8,128)(2,1)} %copy.39), calls=%async_computation.3 | async-start | bytes 2211840 | tf_op jit(solution)/shard_map/all_to_all | solution.py:73
  78.2 0.8 convolution_bitcast_fusion
  79.1 1.0 convolution_convert_fusion.1
  80.0 12.1 %all-to-all-done.3 = bf16[72,4,1920]{2,0,1:T(8,128)(2,1)S(1)} async-done(((bf16[72,4,1920]{2,0,1:T(8,128)(2,1)}), bf16[72,4,1920]{2,0,1:T(8,128)(2,1)S(1)}, u32[]{:S(2)}, u32[]{:S(2)}) %all-to-all-start.3) | async-done | bytes 1105952 | tf_op jit(solution)/shard_map/all_to_all | solution.py:73
  92.1 8.0 %convert_bitcast_fusion = bf16[1920,2048]{0,1:T(8,128)(2,1)} fusion(bf16[288,2048]{1,0:T(8,128)(2,1)} %all-gather.2.cloned.1.call-done, bf16[288,1920]{1,0:T(8,128)(2,1)S(1)} %bitcast.49), kind=kOutput, calls=%fused_computation | convolution fusion | flops 2268856320 | bytes 10149888 | tf_op jit(solution)/shard_map/dot_general | solution.py:75
  100.1 10.6 %copy.41 = bf16[1920,2048]{1,0:T(8,128)(2,1)} copy(bf16[1920,2048]{0,1:T(8,128)(2,1)} %convert_bitcast_fusion) | data formatting | bytes 15728640
  110.7 91.9 %all-reduce.2.cloned.1.call-done = f32[2048,8]{0,1:T(8,128)} async-done(((f32[2048,8]{0,1:T(8,128)}), f32[2048,8]{0,1:T(8,128)}) %all-reduce.2.cloned.1.call-update) | async-done | bytes 65552 | tf_op jit(solution)/shard_map/psum | solution.py:72
  202.5 1.5 copy.56
  (30 shorter events, 0.8 us)
Async XLA Ops:
  8.0 14.8 %copy-start = (bf16[32,2048]{1,0:T(8,128)(2,1)S(1)}, bf16[32,2048]{1,0:T(8,128)(2,1)}, u32[]{:S(2)}) copy-start(bf16[32,2048]{1,0:T(8,128)(2,1)} %param.11) | copy-start | bytes 393220
  8.0 7.4 %all-to-all-start = ((bf16[2,32,1024]{2,1,0:T(8,128)(2,1)}), bf16[2,32,1024]{2,1,0:T(8,128)(2,1)S(1)}, u32[]{:S(2)}, u32[]{:S(2)}) async-start(bf16[2,32,1024]{2,1,0:T(8,128)(2,1)} %bitcast.51), calls=%async_computation | async-start | bytes 262144 | tf_op jit(solution)/shard_map/all_to_all | solution.py:17
  18.0 10.1 %all-to-all-start.1 = ((bf16[8,1,9]{2,1,0:T(2,128)(2,1)}), bf16[8,1,9]{2,1,0:T(2,128)(2,1)S(1)}, u32[]{:S(2)}, u32[]{:S(2)}) async-start(bf16[8,1,9]{2,1,0:T(2,128)(2,1)} %copy.37), calls=%async_computation.1 | async-start | bytes 8192 | tf_op jit(solution)/shard_map/all_to_all | solution.py:45
  23.9 19.1 %copy-start.1 = (bf16[1,72,7680]{2,1,0:T(8,128)(2,1)S(1)}, bf16[1,72,7680]{2,1,0:T(8,128)(2,1)}, u32[]{:S(2)}) copy-start(bf16[1,72,7680]{2,1,0:T(8,128)(2,1)} %param.10) | copy-start | bytes 3317764
  28.1 13.9 %all-to-all-start.2 = ((bf16[8,9,2048]{2,1,0:T(8,128)(2,1)}), bf16[8,9,2048]{2,1,0:T(8,128)(2,1)S(1)}, u32[]{:S(2)}, u32[]{:S(2)}) async-start(bf16[8,9,2048]{2,1,0:T(8,128)(2,1)} %convolution_convert_fusion), calls=%async_computation.2 | async-start | bytes 1048576 | tf_op jit(solution)/shard_map/all_to_all | solution.py:44
  31.6 60.5 %all-gather.2.cloned.1.call-start = ((), (), s32[]{:S(2)}) async-start(), calls=%async_computation.5 | async-start | bytes 1474560 | tf_op jit(solution)/shard_map/all_gather | solution.py:74
  59.5 11.9 %all-to-all-start.4 = ((f32[8,1,9]{2,1,0:T(1,128)}), f32[8,1,9]{2,1,0:T(1,128)S(1)}, u32[]{:S(2)}, u32[]{:S(2)}) async-start(f32[8,1,9]{2,1,0:T(1,128)} %bitcast.13), calls=%async_computation.4 | async-start | bytes 8192 | tf_op jit(solution)/shard_map/all_to_all | solution.py:58
  67.5 10.7 %copy-start.3 = (s32[32,2]{0,1:T(2,128)S(1)}, s32[32,2]{0,1:T(2,128)}, u32[]{:S(2)}) copy-start(s32[32,2]{0,1:T(2,128)} %param.8) | copy-start | bytes 772
  67.5 11.6 %copy-start.2 = (bf16[2048,8]{0,1:T(8,128)(2,1)S(1)}, bf16[2048,8]{0,1:T(8,128)(2,1)}, u32[]{:S(2)}) copy-start(bf16[2048,8]{0,1:T(8,128)(2,1)} %param.7) | copy-start | bytes 98308
  71.3 20.8 %all-to-all-start.3 = ((bf16[72,4,1920]{2,0,1:T(8,128)(2,1)}), bf16[72,4,1920]{2,0,1:T(8,128)(2,1)S(1)}, u32[]{:S(2)}, u32[]{:S(2)}) async-start(bf16[72,4,1920]{2,0,1:T(8,128)(2,1)} %copy.39), calls=%async_computation.3 | async-start | bytes 2211840 | tf_op jit(solution)/shard_map/all_to_all | solution.py:73
  78.0 124.6 %all-reduce.2.cloned.1.call-start = ((), (), s32[]{:S(2)}) async-start(), calls=%async_computation.6 | async-start | bytes 131072 | tf_op jit(solution)/shard_map/psum | solution.py:72
Sparse Core Ops, SparseCore 0:
  43.1 21.1 all-gather.1
Sparse Core Ops, SparseCore 1:
  84.6 117.9 all-reduce.1
where the time goes:
time: 212 us; the launch traced here: 211 us
  waiting for transfers between devices  124 us (58%)
  matrix products  27.6 us (13%)
  starting transfers between devices  25.2 us (12%)
  local copies, waits for them, and re-layouts  16.3 us (8%)
  between operations  15.6 us (7%)
  other arithmetic  2.78 us (1%)
    psum x1, waiting for transfers between devices, per_device(): router_grad = lax.psum(router_local, ('dp', 'expert', 'tensor'))  91.9 us
    dot_general x1, matrix products, per_device(): lax.dot_general(recv_grad, down_weight, (((1,), (1,)), ((), ())), preferr...  15.7 us
    unnamed x12, local copies, waits for them, and re-layouts  13 us
    all_to_all x1, waiting for transfers between devices, per_device(): lax.all_to_all(hidden_rows, 'dp', split_axis=1, concat_axis=0, tiled=True)  12.1 us
    all_to_all x1, waiting for transfers between devices, per_device(): lax.all_to_all(send_grad, ('expert', 'tensor'), split_axis=0, concat_axis...  10.3 us
    dot_general x1, matrix products, per_device(): lax.dot_general(hidden_all, gated_all, (((0,), (0,)), ((), ())), preferre...  7.96 us
    all_to_all x1, starting transfers between devices, per_device(): lax.all_to_all(hidden_rows, 'dp', split_axis=1, concat_axis=0, tiled=True)  6.66 us
    all_to_all x1, starting transfers between devices, per_device(): lax.all_to_all(gate_partial, ('expert', 'tensor'), split_axis=0, concat_a...  6.6 us
  transfers between devices with their start and end apart: 7, of which 6 were waited for; matrix products, arithmetic and copies ran while one was open for 19% of the time, Pallas kernels for 0%

commit v1 on v0

--- a/solution.py
+++ b/solution.py
@@ -70,7 +70,10 @@
         full_input.astype(jnp.float32).T, logit_grad, precision=lax.Precision.HIGHEST
     )
     router_grad = lax.psum(router_local, ("dp", "expert", "tensor"))
-    hidden_all = lax.all_to_all(hidden_rows, "dp", split_axis=1, concat_axis=0, tiled=True)
+    hidden_all = jnp.concatenate(
+        lax.all_to_all(jnp.stack(jnp.split(hidden_rows, lax.axis_size("dp"), axis=1)), "dp", 0, 0),
+        axis=0,
+    )
     gated_all = lax.all_gather(gated_grad, "dp", axis=0, tiled=True)
     weight_sum = lax.dot_general(
         hidden_all, gated_all, (((0,), (0,)), ((), ())), preferred_element_type=jnp.float32

time: 212 us -> 212 us (level)
  local copies, waits for them, and re-layouts: 16.3 us -> 4.34 us
  waiting for transfers between devices: 124 us -> 135 us
    psum x1, waiting for transfers between devices: 91.9 us -> 103 us  [per_device(): router_grad = lax.psum(router_local, ('dp', 'expert', 'tensor'))]
    unnamed x12 -> x11, local copies, waits for them, and re-layouts: 13 us -> 2.34 us
  transfers between devices with their start and end apart: 7 -> 7, of which waited for: 6 -> 6; matrix products, arithmetic and copies ran while one was open for 19% -> 14% of each run, Pallas kernels for 0% -> 0%
where the time goes in v1:
time: 212 us
  waiting for transfers between devices  135 us (64%)
  matrix products  27.2 us (13%)
  starting transfers between devices  25.2 us (12%)
  between operations  15.6 us (7%)
  local copies, waits for them, and re-layouts  4.34 us (2%)
  other arithmetic  3.95 us (2%)
    psum x1, waiting for transfers between devices, per_device(): router_grad = lax.psum(router_local, ('dp', 'expert', 'tensor'))  103 us
    dot_general x1, matrix products, per_device(): lax.dot_general(recv_grad, down_weight, (((1,), (1,)), ((), ())), preferr...  15.7 us
    all_to_all x1, waiting for transfers between devices, per_device(): lax.all_to_all(jnp.stack(jnp.split(hidden_rows, lax.axis_size('dp'), axis...  12.1 us
    all_to_all x1, waiting for transfers between devices, per_device(): lax.all_to_all(send_grad, ('expert', 'tensor'), split_axis=0, concat_axis...  10.2 us
    dot_general x1, matrix products, per_device(): lax.dot_general(hidden_all, gated_all, (((0,), (0,)), ((), ())), preferre...  7.47 us
    all_to_all x1, starting transfers between devices, per_device(): lax.all_to_all(jnp.stack(jnp.split(hidden_rows, lax.axis_size('dp'), axis...  6.66 us
    all_to_all x1, starting transfers between devices, per_device(): lax.all_to_all(gate_partial, ('expert', 'tensor'), split_axis=0, concat_a...  6.6 us
    all_to_all x1, starting transfers between devices, per_device(): lax.all_to_all(send_gate, ('expert', 'tensor'), split_axis=0, concat_axis...  4.86 us
  transfers between devices with their start and end apart: 7, of which 6 were waited for; matrix products, arithmetic and copies ran while one was open for 14% of the time, Pallas kernels for 0%

profile of v1, /device:TPU:1, one launch (start us, length us, event | category | flops | bytes accessed | tf_op | source)
XLA Modules:
  0.0 211.6 jit_solution(4608438540375382982)
XLA Ops:
  8.0 3.5 %all-to-all-start.1 = ((bf16[2,32,1024]{2,1,0:T(8,128)(2,1)}), bf16[2,32,1024]{2,1,0:T(8,128)(2,1)S(1)}, u32[]{:S(2)}, u32[]{:S(2)}) async-start(bf16[2,32,1024]{2,1,0:T(8,128)(2,1)} %bitcast.55), calls=%async_computation.1 | async-start | bytes 262144 | tf_op jit(solution)/shard_map/all_to_all | solution.py:17
  11.5 0.8 copy.24
  12.3 0.7 convert_convert_fusion
  13.0 0.1 eq.49
  13.2 0.1 reduce_window_sum.11
  13.3 0.2 select_reduce_fusion
  13.4 0.1 eq.53
  13.7 1.7 all-to-all-done.1
  15.4 1.0 fusion.13
  16.4 0.7 multiply_reduce_fusion.3
  17.2 0.2 fusion.1
  17.3 0.1 copy.31
  17.4 0.6 copy.27
  18.1 4.9 %all-to-all-start.2 = ((bf16[8,1,9]{2,1,0:T(2,128)(2,1)}), bf16[8,1,9]{2,1,0:T(2,128)(2,1)S(1)}, u32[]{:S(2)}, u32[]{:S(2)}) async-start(bf16[8,1,9]{2,1,0:T(2,128)(2,1)} %copy.27), calls=%async_computation.2 | async-start | bytes 8192 | tf_op jit(solution)/shard_map/all_to_all | solution.py:45
  22.9 1.1 convolution_convert_fusion.1
  24.0 4.2 %all-to-all-done.2 = bf16[8,1,9]{2,1,0:T(2,128)(2,1)S(1)} async-done(((bf16[8,1,9]{2,1,0:T(2,128)(2,1)}), bf16[8,1,9]{2,1,0:T(2,128)(2,1)S(1)}, u32[]{:S(2)}, u32[]{:S(2)}) %all-to-all-start.2) | async-done | bytes 176 | tf_op jit(solution)/shard_map/all_to_all | solution.py:45
  28.2 3.5 %all-to-all-start.3 = ((bf16[8,9,2048]{2,1,0:T(8,128)(2,1)}), bf16[8,9,2048]{2,1,0:T(8,128)(2,1)S(1)}, u32[]{:S(2)}, u32[]{:S(2)}) async-start(bf16[8,9,2048]{2,1,0:T(8,128)(2,1)} %convolution_convert_fusion.1), calls=%async_computation.3 | async-start | bytes 1048576 | tf_op jit(solution)/shard_map/all_to_all | solution.py:44
  32.0 10.2 %all-to-all-done.3 = bf16[8,9,2048]{2,1,0:T(8,128)(2,1)S(1)} async-done(((bf16[8,9,2048]{2,1,0:T(8,128)(2,1)}), bf16[8,9,2048]{2,1,0:T(8,128)(2,1)S(1)}, u32[]{:S(2)}, u32[]{:S(2)}) %all-to-all-start.3) | async-done | bytes 294944 | tf_op jit(solution)/shard_map/all_to_all | solution.py:44
  42.1 0.1 reshape.58
  42.3 0.8 multiply_convert_fusion.1
  43.1 15.7 %multiply_reduce_fusion = (f32[72]{0:T(128)S(1)}, bf16[1,72,7680]{2,1,0:T(8,128)(2,1)}) fusion(bf16[1,72,7680]{2,1,0:T(8,128)(2,1)S(1)} %copy-done.1, f32[72]{0:T(128)S(1)} %reshape.59, bf16[72,2048]{1,0:T(8,128)(2,1)S(1)} %reshape.58, bf16[7680,2048]{1,0:T(8,128)(2,1)} %param.9), kind=kOutput, calls=%fused_computation.4 | convolution fusion | flops 2267688960 | bytes 33964608 | tf_op jit(solution)/shard_map/dot_general | solution.py:51
  58.9 0.7 all_to_all.40
  59.6 6.6 %all-to-all-start.4 = ((f32[8,1,9]{2,1,0:T(1,128)}), f32[8,1,9]{2,1,0:T(1,128)S(1)}, u32[]{:S(2)}, u32[]{:S(2)}) async-start(f32[8,1,9]{2,1,0:T(1,128)} %bitcast.15), calls=%async_computation.4 | async-start | bytes 8192 | tf_op jit(solution)/shard_map/all_to_all | solution.py:58
  66.2 1.2 pad_maximum_fusion
  67.3 4.1 %all-to-all-done.4 = f32[8,1,9]{2,1,0:T(1,128)S(1)} async-done(((f32[8,1,9]{2,1,0:T(1,128)}), f32[8,1,9]{2,1,0:T(1,128)S(1)}, u32[]{:S(2)}, u32[]{:S(2)}) %all-to-all-start.4) | async-done | bytes 320 | tf_op jit(solution)/shard_map/all_to_all | solution.py:58
  71.4 6.7 %all-to-all-start = ((bf16[4,72,1920]{2,1,0:T(8,128)(2,1)}), bf16[4,72,1920]{2,1,0:T(8,128)(2,1)S(1)}, u32[]{:S(2)}, u32[]{:S(2)}) async-start(bf16[4,72,1920]{2,1,0:T(8,128)(2,1)} %pad_maximum_fusion), calls=%async_computation | async-start | bytes 2211840 | tf_op jit(solution)/shard_map/all_to_all | solution.py:74
  78.3 0.8 convolution_bitcast_fusion
  79.2 1.0 convolution_convert_fusion.2
  80.1 12.1 %all-to-all-done = bf16[4,72,1920]{2,1,0:T(8,128)(2,1)S(1)} async-done(((bf16[4,72,1920]{2,1,0:T(8,128)(2,1)}), bf16[4,72,1920]{2,1,0:T(8,128)(2,1)S(1)}, u32[]{:S(2)}, u32[]{:S(2)}) %all-to-all-start) | async-done | bytes 1105952 | tf_op jit(solution)/shard_map/all_to_all | solution.py:74
  92.2 7.5 %convolution_convert_fusion = bf16[1920,2048]{1,0:T(8,128)(2,1)} fusion(bf16[288,1920]{1,0:T(8,128)(2,1)S(1)} %bitcast.53, bf16[288,2048]{1,0:T(8,128)(2,1)} %all-gather.2.cloned.1.call-done), kind=kOutput, calls=%fused_computation | convolution fusion | flops 2268856320 | bytes 10149888 | tf_op jit(solution)/shard_map/dot_general | solution.py:78
  99.7 103.0 %all-reduce.2.cloned.1.call-done = f32[2048,8]{0,1:T(8,128)} async-done(((f32[2048,8]{0,1:T(8,128)}), f32[2048,8]{0,1:T(8,128)}) %all-reduce.2.cloned.1.call-update) | async-done | bytes 65552 | tf_op jit(solution)/shard_map/psum | solution.py:72
  202.6 1.5 copy.44
  (29 shorter events, 0.7 us)
Async XLA Ops:
  8.0 14.9 %copy-start = (bf16[32,2048]{1,0:T(8,128)(2,1)S(1)}, bf16[32,2048]{1,0:T(8,128)(2,1)}, u32[]{:S(2)}) copy-start(bf16[32,2048]{1,0:T(8,128)(2,1)} %param.11) | copy-start | bytes 393220
  8.0 7.4 %all-to-all-start.1 = ((bf16[2,32,1024]{2,1,0:T(8,128)(2,1)}), bf16[2,32,1024]{2,1,0:T(8,128)(2,1)S(1)}, u32[]{:S(2)}, u32[]{:S(2)}) async-start(bf16[2,32,1024]{2,1,0:T(8,128)(2,1)} %bitcast.55), calls=%async_computation.1 | async-start | bytes 262144 | tf_op jit(solution)/shard_map/all_to_all | solution.py:17
  15.4 16.3 %copy-start.1 = (bf16[1,72,7680]{2,1,0:T(8,128)(2,1)S(1)}, bf16[1,72,7680]{2,1,0:T(8,128)(2,1)}, u32[]{:S(2)}) copy-start(bf16[1,72,7680]{2,1,0:T(8,128)(2,1)} %param.10) | copy-start | bytes 3317764
  18.1 10.1 %all-to-all-start.2 = ((bf16[8,1,9]{2,1,0:T(2,128)(2,1)}), bf16[8,1,9]{2,1,0:T(2,128)(2,1)S(1)}, u32[]{:S(2)}, u32[]{:S(2)}) async-start(bf16[8,1,9]{2,1,0:T(2,128)(2,1)} %copy.27), calls=%async_computation.2 | async-start | bytes 8192 | tf_op jit(solution)/shard_map/all_to_all | solution.py:45
  28.2 13.9 %all-to-all-start.3 = ((bf16[8,9,2048]{2,1,0:T(8,128)(2,1)}), bf16[8,9,2048]{2,1,0:T(8,128)(2,1)S(1)}, u32[]{:S(2)}, u32[]{:S(2)}) async-start(bf16[8,9,2048]{2,1,0:T(8,128)(2,1)} %convolution_convert_fusion.1), calls=%async_computation.3 | async-start | bytes 1048576 | tf_op jit(solution)/shard_map/all_to_all | solution.py:44
  31.7 60.5 %all-gather.2.cloned.1.call-start = ((), (), s32[]{:S(2)}) async-start(), calls=%async_computation.5 | async-start | bytes 1474560 | tf_op jit(solution)/shard_map/all_gather | solution.py:77
  59.6 11.9 %all-to-all-start.4 = ((f32[8,1,9]{2,1,0:T(1,128)}), f32[8,1,9]{2,1,0:T(1,128)S(1)}, u32[]{:S(2)}, u32[]{:S(2)}) async-start(f32[8,1,9]{2,1,0:T(1,128)} %bitcast.15), calls=%async_computation.4 | async-start | bytes 8192 | tf_op jit(solution)/shard_map/all_to_all | solution.py:58
  67.3 11.0 %copy-start.3 = (s32[32,2]{0,1:T(2,128)S(1)}, s32[32,2]{0,1:T(2,128)}, u32[]{:S(2)}) copy-start(s32[32,2]{0,1:T(2,128)} %param.8) | copy-start | bytes 772
  67.3 11.8 %copy-start.2 = (bf16[2048,8]{0,1:T(8,128)(2,1)S(1)}, bf16[2048,8]{0,1:T(8,128)(2,1)}, u32[]{:S(2)}) copy-start(bf16[2048,8]{0,1:T(8,128)(2,1)} %param.7) | copy-start | bytes 98308
  71.4 20.8 %all-to-all-start = ((bf16[4,72,1920]{2,1,0:T(8,128)(2,1)}), bf16[4,72,1920]{2,1,0:T(8,128)(2,1)S(1)}, u32[]{:S(2)}, u32[]{:S(2)}) async-start(bf16[4,72,1920]{2,1,0:T(8,128)(2,1)} %pad_maximum_fusion), calls=%async_computation | async-start | bytes 2211840 | tf_op jit(solution)/shard_map/all_to_all | solution.py:74
  78.1 124.6 %all-reduce.2.cloned.1.call-start = ((), (), s32[]{:S(2)}) async-start(), calls=%async_computation.6 | async-start | bytes 131072 | tf_op jit(solution)/shard_map/psum | solution.py:72
Sparse Core Ops, SparseCore 0:
  43.3 21.1 all-gather.1
Sparse Core Ops, SparseCore 1:
  84.7 117.9 all-reduce.1
